TPU v7x, 32 devices: a 4x4x1 block of a 4x4x8 slice. The times are simulated.
32 devices in a mesh: rep: 1 (over z), dp: 32 (over x, y, core).
Axes of the slice: x: 4, y: 4, z: 1, core: 2. Of those that a mesh axis runs over, the one named last changes fastest.
The devices are a block of a 4x4x8 slice.
Arguments:
- x: bfloat16 [32, 2048, 768], P(('rep', 'dp'))
- dy: bfloat16 [32, 2048, 768], P(('rep', 'dp'))
- w_gate: bfloat16 [2, 768, 2048], replicated
- w_up: bfloat16 [2, 768, 2048], replicated
- w_down: bfloat16 [2, 2048, 768], replicated
- m_w_gate: float32 [2, 768, 2048], P(None, 'dp')
- m_w_up: float32 [2, 768, 2048], P(None, 'dp')
- m_w_down: float32 [2, 2048, 768], P(None, 'dp')
- v_w_gate: float32 [2, 768, 2048], P(None, 'dp')
- v_w_up: float32 [2, 768, 2048], P(None, 'dp')
- v_w_down: float32 [2, 2048, 768], P(None, 'dp')
Outputs:
- output 1: bfloat16 [2, 768, 2048], P('rep')
- output 2: bfloat16 [2, 768, 2048], P('rep')
- output 3: bfloat16 [2, 2048, 768], P('rep')
- output 4: float32 [2, 768, 2048], P('rep', 'dp')
- output 5: float32 [2, 768, 2048], P('rep', 'dp')
- output 6: float32 [2, 2048, 768], P('rep', 'dp')
- output 7: float32 [2, 768, 2048], P('rep', 'dp')
- output 8: float32 [2, 768, 2048], P('rep', 'dp')
- output 9: float32 [2, 2048, 768], P('rep', 'dp')
All inputs are finite; a program needn't handle non-finite values.
Results may differ from a plain program's by a relative error of at most 0.022.
Values are sent between devices in bfloat16 or wider.
A program may use at most 768 MiB of HBM per device.

v0:
```python
import functools
import math

import jax
import jax.numpy as jnp
from jax import lax
from jax.experimental import pallas as pl
from jax.experimental.pallas import tpu as pltpu
from jax.sharding import PartitionSpec as P

NAMES = ("w_gate", "w_up", "w_down")
F32, BF16 = jnp.float32, jnp.bfloat16
ANY = pl.BlockSpec(memory_space=pl.ANY)
VM = pl.BlockSpec(memory_space=pltpu.VMEM)
CORES = 2
LAGS = (0, 2, 5, 9, 12, 15)


def contract(a, b, dims):
    return lax.dot_general(a, b, ((dims[:1], dims[1:]), ((), ())), preferred_element_type=F32)


def rms_scale(wide):
    return lax.rsqrt(jnp.mean(wide**2, -1, keepdims=True) + 1e-6)


def sigmoid(t):
    return 0.5 * jnp.tanh(0.5 * t) + 0.5


def states_kernel(steps, chunk_f, *refs):
    x, dy, *weights = refs[:5]
    big_out = refs[5:11]
    at0, at1, dh_out = refs[11:14]
    vw, gate0, up0, bufs, wsem, osem = refs[14], refs[15], refs[16], refs[17], refs[18], refs[19]
    t = pl.program_id(0)
    rows = x.shape[1]
    ff = gate0.shape[1]
    layers = weights[0].shape[0]

    def load(k, l):
        dst = vw[k].at[l]
        return pltpu.make_async_copy(weights[k].at[l], dst, wsem.at[k, l])

    @pl.when(t == 0)
    def _():
        for k in range(3):
            load(k, 0).start()

    def need(k, l):
        @pl.when(t == 0)
        def _():
            load(k, l).wait()

    def put(i, tile):
        return pltpu.make_async_copy(bufs.at[i], big_out[i].at[pl.ds(tile * rows, rows)], osem.at[i])

    def free(i):
        @pl.when(t > 0)
        def _():
            put(i, t - 1).wait()

    def parts():
        return [pl.ds(j, chunk_f) for j in range(0, ff, chunk_f)]

    def back(j, dp, g, u, to_gate, to_up):
        sig = sigmoid(g)
        silu = g * sig
        bufs[to_up, :, j] = (dp * silu).astype(BF16)
        bufs[to_gate, :, j] = (dp * u * (sig * (1.0 + g * (1.0 - sig)))).astype(BF16)
        return silu

    h0 = x[0]
    wide = h0.astype(F32)
    a0 = (wide * rms_scale(wide)).astype(BF16)
    at0[...] = a0.T
    need(0, 0)
    need(1, 0)

    @pl.when(t == 0)
    def _():
        for l in range(1, layers):
            for k in range(3):
                load(k, l).start()

    free(0)
    for j in parts():
        g = contract(a0, vw[0][0, :, j], (1, 0))
        u = contract(a0, vw[1][0, :, j], (1, 0))
        gate0[:, j] = g
        up0[:, j] = u
        bufs[0, :, j] = (g * sigmoid(g) * u).astype(BF16)
    put(0, t).start()
    need(2, 0)
    y = contract(bufs[0], vw[2][0], (1, 0)).astype(BF16)
    h1 = (wide + y.astype(F32)).astype(BF16)

    wide = h1.astype(F32)
    scale = rms_scale(wide)
    a1 = (wide * scale).astype(BF16)
    at1[...] = a1.T
    for k in range(3):
        need(k, 1)
    for i in (1, 2, 3):
        free(i)
    d = dy[0]
    for j in parts():
        g = contract(a1, vw[0][1, :, j], (1, 0))
        u = contract(a1, vw[1][1, :, j], (1, 0))
        dp = contract(d, vw[2][1, j, :], (1, 1)).astype(BF16).astype(F32)
        silu = back(j, dp, g, u, 2, 3)
        bufs[1, :, j] = (silu * u).astype(BF16)
    for i in (1, 2, 3):
        put(i, t).start()
    da = contract(bufs[2], vw[0][1], (1, 1)).astype(BF16).astype(F32)
    da = da + contract(bufs[3], vw[1][1], (1, 1)).astype(BF16).astype(F32)
    da = da.astype(BF16).astype(F32)
    inner = jnp.mean(da * wide, -1, keepdims=True)
    dwide = da * scale - wide * (scale * scale * scale * inner)
    dh = (d.astype(F32) + dwide.astype(BF16).astype(F32)).astype(BF16)
    dh_out[...] = dh

    for i in (4, 5):
        free(i)
    for j in parts():
        dp = contract(dh, vw[2][0, j, :], (1, 1)).astype(BF16).astype(F32)
        back(j, dp, gate0[:, j], up0[:, j], 4, 5)
    for i in (4, 5):
        put(i, t).start()

    @pl.when(t == steps - 1)
    def _():
        for i in range(6):
            put(i, t).wait()


def states_body(steps, chunk_f, *refs):
    vw = refs[14:17]
    states_kernel(steps, chunk_f, *refs[:14], vw, *refs[17:])


def states(x, dy, weights):
    _, tokens, d = x.shape
    ff = weights[0].shape[2]
    tile = min(512, tokens)
    steps = tokens // tile
    seq = pl.BlockSpec((1, tile, d), lambda i: (0, i, 0))
    across = pl.BlockSpec((d, tile), lambda i: (0, i))
    out = [jax.ShapeDtypeStruct((tokens, ff), BF16)] * 6
    out += [jax.ShapeDtypeStruct((d, tokens), BF16)] * 2 + [jax.ShapeDtypeStruct((tokens, d), BF16)]
    flops = 2 * tokens * d * ff * 9
    return pl.pallas_call(
        functools.partial(states_body, steps, min(512, ff)),
        grid=(steps,),
        out_shape=out,
        in_specs=[seq, seq, ANY, ANY, ANY],
        out_specs=[ANY] * 6 + [across, across, pl.BlockSpec((tile, d), lambda i: (i, 0))],
        scratch_shapes=[pltpu.VMEM(w.shape, BF16) for w in weights]
        + [
            pltpu.VMEM((tile, ff), F32),
            pltpu.VMEM((tile, ff), F32),
            pltpu.VMEM((6, tile, ff), BF16),
            pltpu.SemaphoreType.DMA((3, weights[0].shape[0])),
            pltpu.SemaphoreType.DMA((6,)),
        ],
        compiler_params=pltpu.CompilerParams(vmem_limit_bytes=63 * 2**20, dimension_semantics=("arbitrary",)),
        cost_estimate=pl.CostEstimate(flops=flops, bytes_accessed=100 * 2**20, transcendentals=0),
        name="states",
    )(x, dy, *weights)


class Place:
    def __init__(self, n):
        self.n, self.side = n, math.isqrt(n // CORES)
        side = self.side
        me = lax.axis_index("dp")
        chip = lax.div(me, CORES)
        self.me = me
        self.core = lax.rem(me, CORES)
        self.x, self.y = lax.div(chip, side), lax.rem(chip, side)
        self.xy = (self.x, self.y)
        self.sibling = me + 1 - 2 * self.core

    def at(self, axis, step):
        return lax.rem(self.xy[axis] + step, self.side)

    def device(self, axis, step):
        to = list(self.xy)
        to[axis] = self.at(axis, step)
        return (to[0] * self.side + to[1]) * CORES + self.core


def chunk(color, p, q):
    return (p, q) if color == 0 else (q, p)


def tail_kernel(n, slabs, count, *refs):
    place = Place(n)
    side = place.side
    ns = len(slabs)
    at_in, an_in = refs[0:2], refs[2:4]
    b_in = (refs[4:6], refs[6:8], refs[8:10])
    w_in, m_in, v_in = (refs[i : i + 3] for i in (10, 13, 16))
    w_out, m_out, v_out = (refs[i : i + 3] for i in (19, 22, 25))
    refs = refs[28:]
    per = {}
    for name in ("full", "d2d", "g", "wo", "mo", "vo", "nw", "pbuf", "qbuf"):
        per[name], refs = refs[:ns], refs[ns:]
    pbuf, qbuf = per["pbuf"], per["qbuf"]
    at, an, btile, ssq, ssq_in, s_send, s_recv, a_send, a_recv, lsem, tsem_s, tsem_r, losem, asem, bsem = refs
    last = side - 1

    def remote(src, dst, send, recv, device):
        return pltpu.make_async_remote_copy(
            src_ref=src, dst_ref=dst, send_sem=send, recv_sem=recv,
            device_id={"dp": device}, device_id_type=pl.DeviceIdType.MESH,
        )

    barrier = pltpu.get_barrier_semaphore()
    partners = [place.sibling] + [place.device(a, s) for a in (0, 1) for s in range(1, side)]
    for d in partners:
        pl.semaphore_signal(barrier, inc=1, device_id={"dp": d}, device_id_type=pl.DeviceIdType.MESH)

    tiles = side
    tile = btile.shape[2]
    slots = btile.shape[0]

    def fetch(s, i):
        k, l = slabs[s][:2]
        slot = (s * tiles + i) % slots if isinstance(i, int) else lax.rem(s * tiles + i, slots)
        return pltpu.make_async_copy(b_in[k][l].at[:, pl.ds(i * tile, tile)], btile.at[slot], bsem.at[slot])

    def load_a(kind, l):
        src, dst = ((an_in[l], an), (at_in[l], at))[kind]
        return pltpu.make_async_copy(src, dst, asem.at[kind])

    top = slabs[0][1]
    load_a(1, top).start()
    fetch(0, 0).start()
    fetch(0, 1).start()
    load_a(0, top).start()
    held = [None, None]
    ssq[0] = jnp.zeros_like(ssq[0])
    local = [[] for _ in range(ns)]
    for s, (k, l, r, c) in enumerate(slabs):
        for j, (src, name) in enumerate(((w_in, "wo"), (m_in, "mo"), (v_in, "vo"))):
            view = src[k].at[l, place.x, place.y, place.core] if j == 0 else src[k].at[l]
            cp = pltpu.make_async_copy(view, per[name][s], lsem.at[s, j])
            cp.start()
            local[s].append(cp)

    def items(s):
        return range(2 if slabs[s][0] == 2 else tiles)

    def cols(s, c):
        width = slabs[s][3] // len(items(s))
        return pl.ds(c * width, width)

    def spot_in(s, c, p, q):
        i, j = chunk(c % 2, p, q)
        return per["full"][s].at[i, j, place.core, :, cols(s, c)]

    def term(s, c, p, q):
        i, j = chunk(c % 2, p, q)
        return spot_in(s, c, p, q)[...].astype(F32) + per["d2d"][s][i, j, :, cols(s, c)].astype(F32)

    def way(s):
        return 1 if s % 2 == 0 else last

    def wire(s, c, slot):
        h = side // 2
        b, b2 = pbuf[s].at[c], qbuf[s].at[c]
        opp = place.at(c % 2, 2)
        if slot == 0:
            ends = spot_in(s, c, opp, pl.ds(0, h)), b.at[0, pl.ds(0, h)], place.device(c % 2, 1)
        elif slot == 1:
            ends = spot_in(s, c, opp, pl.ds(h, h)), b.at[0, pl.ds(h, h)], place.device(c % 2, last)
        elif slot in (2, 3):
            step = 1 if slot == 2 else last
            ends = spot_in(s, c, place.at(c % 2, step), slice(None)), b.at[slot - 1], place.device(c % 2, step)
        elif slot == 4:
            ends = b2.at[0], b2.at[3], place.device(1 - c % 2, way(s))
        elif slot in (5, 6):
            ends = b2.at[slot - 4], b2.at[slot - 1], place.device(1 - c % 2, 1 if slot == 5 else last)
        else:
            ends = per["full"][s].at[:, :, 1 - place.core, :, cols(s, c)], per["d2d"][s].at[:, :, :, cols(s, c)], place.sibling
        return remote(*ends[:2], s_send.at[s, c, slot], s_recv.at[s, c, slot], ends[2])

    def st0(s, c):
        wire(s, c, 7).start()

    def st1(s, c):
        wire(s, c, 7).wait_recv()
        b = pbuf[s].at[c]
        opp = place.at(c % 2, 2)

        @pl.loop(0, side)
        def _(q):
            spot_in(s, c, opp, q)[...] = term(s, c, opp, q).astype(BF16)

        h = side // 2
        wire(s, c, 0).start()
        wire(s, c, 1).start()

    def st2(s, c):
        h = side // 2
        b = pbuf[s].at[c]
        for slot, step, lo in ((2, 1, 0), (3, last, h)):
            wire(s, c, slot - 2).wait_recv()
            to = place.at(c % 2, step)

            @pl.loop(0, h)
            def _(q, to=to, lo=lo):
                z = term(s, c, to, lo + q) + b[0, lo + q].astype(F32)
                spot_in(s, c, to, lo + q)[...] = z.astype(BF16)
                spot_in(s, c, to, h - lo + q)[...] = term(s, c, to, h - lo + q).astype(BF16)

            wire(s, c, slot).start()

    def psum(s, c, q):
        b = pbuf[s].at[c]
        return term(s, c, place.xy[c % 2], q) + b[1, q].astype(F32) + b[2, q].astype(F32)

    def st3(s, c):
        wire(s, c, 2).wait_recv()
        wire(s, c, 3).wait_recv()
        b = qbuf[s].at[c]
        b[0] = psum(s, c, place.at(1 - c % 2, 2)).astype(BF16)
        wire(s, c, 4).start()

    def st4(s, c):
        b = qbuf[s].at[c]
        wire(s, c, 4).wait_recv()
        for slot, step, to in ((1, 1, 4), (2, last, 5)):
            z = psum(s, c, place.at(1 - c % 2, step))
            b[slot] = (z + b[3].astype(F32) if step == way(s) else z).astype(BF16)
            wire(s, c, 4 + slot).start()

    def st5(s, c):
        rows, columns = slabs[s][2:]
        b = qbuf[s].at[c]
        wire(s, c, 5).wait_recv()
        wire(s, c, 6).wait_recv()
        z = psum(s, c, place.xy[1 - c % 2]) + b[4].astype(F32) + b[5].astype(F32)
        z = z.astype(BF16).astype(F32)
        per["g"][s][:, cols(s, c)] = z
        sq = z * z
        tot = None
        for i in range(0, rows, 8):
            for j in range(0, columns // len(items(s)), 128):
                part = sq[i : i + 8, j : j + 128]
                tot = part if tot is None else tot + part
        ssq[0] = ssq[0] + tot

    stages = (st0, st1, st2, st3, st4, st5)
    events = []
    for s, (k, l, r, columns) in enumerate(slabs):
        for c in items(s):
            ready = s * tiles + (tiles if k == 2 else c + 1)
            events += [(ready + LAGS[i], i, s, c) for i in range(len(stages))]
    events.sort()

    def run(time):
        for when, i, s, c in events:
            if when == time:
                stages[i](s, c)

    for s, (k, l, r, columns) in enumerate(slabs):
        if s == 0:
            pl.semaphore_wait(barrier, len(partners))
        run(s * tiles)
        kind = 0 if k == 2 else 1
        if held[kind] != l:
            load_a(kind, l).wait()
            held[kind] = l

        @pl.loop(0, tiles)
        def _(i, s=s, k=k, r=r, columns=columns):
            for other in range(1, tiles):
                if any(e[0] == s * tiles + other for e in events):
                    pl.when(i == other)(functools.partial(run, s * tiles + other))
            fetch(s, i).wait()

            @pl.when(i < tiles - 2)
            def _():
                fetch(s, i + 2).start()

            if s + 1 < ns:

                @pl.when(i >= tiles - 2)
                def _():
                    fetch(s + 1, i - (tiles - 2)).start()

            slot = (s * tiles + i) % slots if isinstance(i, int) else lax.rem(s * tiles + i, slots)
            if k == 2:
                z = contract(btile[slot], an[...], (0, 0))
                per["full"][s][i] = z.reshape(side, CORES, r, columns).astype(BF16)
            else:
                z = contract(at[...], btile[slot], (1, 0))
                z = z.reshape(side, side, CORES, r, tile).astype(BF16)
                per["full"][s][:, :, :, :, pl.ds(pl.multiple_of(i * tile, tile), tile)] = z

        if l > 0 and not any((k2 == 2) == (k == 2) and l2 == l for k2, l2, _, _ in slabs[s + 1 :]):
            load_a(kind, l - 1).start()
    for time in range(ns * tiles, events[-1][0] + 1):
        run(time)

    sends = []
    slot = 0
    for axis in (None, 0, 1):
        steps = (0,) if axis is None else range(1, side)
        mine = []
        for st in steps:
            device = place.sibling if axis is None else place.device(axis, st)
            cp = remote(ssq.at[0 if axis is None else axis + 1], ssq_in.at[slot], tsem_s.at[slot], tsem_r.at[slot], device)
            cp.start()
            mine.append((cp, slot))
            sends.append(cp)
            slot += 1
        z = ssq[0 if axis is None else axis + 1]
        for cp, sl in mine:
            cp.wait_recv()
            z = z + ssq_in[sl]
        ssq[1 if axis is None else axis + 2] = z
    total = jnp.sum(ssq[3], axis=(0, 1), keepdims=True)
    factor = jnp.minimum(1.0, 0.5 * lax.rsqrt(total / count + 1e-30))

    apend = {}

    def asend(s, c, slot, src, dst, device):
        cp = remote(src, dst, a_send.at[s, c, slot], a_recv.at[s, c, slot], device)
        cp.start()
        apend[s, c, slot] = cp

    def half(s, c):
        width = slabs[s][3] // 2
        return pl.ds(c * width, width)

    def spot(s, c, p, q):
        k, l = slabs[s][:2]
        i, j = chunk(c, p, q)
        return w_out[k].at[l, i, j, place.core, :, half(s, c)]

    outs = []

    def a0(s):
        k, l, rows, columns = slabs[s]
        for cp in local[s]:
            cp.wait()
        for i in range(0, rows, 8):
            here = (pl.ds(i, 8), slice(None))
            g = per["g"][s][here] * factor
            m = 0.9 * per["mo"][s][here] + 0.1 * g
            v = 0.95 * per["vo"][s][here] + 0.05 * g * g
            w = per["wo"][s][here].astype(F32)
            step = m * lax.rsqrt(v + 1e-8) + 0.1 * w
            per["mo"][s][here] = m
            per["vo"][s][here] = v
            per["nw"][s][here] = (w - 0.02 * step).astype(BF16)
        for j, (src, dst) in enumerate(((per["nw"], w_out[k].at[l, place.x, place.y, place.core]), (per["mo"], m_out[k].at[l]), (per["vo"], v_out[k].at[l]))):
            cp = pltpu.make_async_copy(src[s], dst, losem.at[s, j])
            cp.start()
            outs.append(cp) if j else local[s].append(cp)
        for c in (0, 1):
            p, q = place.xy[c], place.xy[1 - c]
            mine = per["nw"][s].at[:, half(s, c)]
            asend(s, c, 0, mine, spot(s, c, p, q), place.device(1 - c, 1))
            asend(s, c, 1, mine, spot(s, c, p, q), place.device(1 - c, last))

    def a1(s):
        step = way(s)
        for c in (0, 1):
            apend[s, c, 0].wait_recv()
            apend[s, c, 1].wait_recv()
            block = spot(s, c, place.xy[c], place.at(1 - c, side - step))
            asend(s, c, 2, block, block, place.device(1 - c, step))

    def a2(s):
        local[s][-1].wait()
        for c in (0, 1):
            apend[s, c, 2].wait_recv()
            row = spot(s, c, place.xy[c], slice(None))
            asend(s, c, 3, row, row, place.device(c, 1))
            asend(s, c, 4, row, row, place.device(c, last))
            asend(s, c, 7, row, row, place.sibling)

    def a3(s):
        h = side // 2
        for c in (0, 1):
            apend[s, c, 3].wait_recv()
            left = spot(s, c, place.at(c, last), pl.ds(0, h))
            asend(s, c, 5, left, left, place.device(c, 1))
            apend[s, c, 4].wait_recv()
            right = spot(s, c, place.at(c, 1), pl.ds(h, h))
            asend(s, c, 6, right, right, place.device(c, last))
            for slot, step in ((8, last), (9, 1)):
                row = spot(s, c, place.at(c, step), slice(None))
                asend(s, c, slot, row, row, place.sibling)

    def a4(s):
        for c in (0, 1):
            apend[s, c, 5].wait_recv()
            apend[s, c, 6].wait_recv()
            row = spot(s, c, place.at(c, 2), slice(None))
            asend(s, c, 10, row, row, place.sibling)

    stages = (a0, a1, a2, a3, a4)
    for t in range(ns + len(stages) - 1):
        for i, st in enumerate(stages):
            if 0 <= t - i < ns:
                st(t - i)
    for s in range(ns):
        for c in (0, 1):
            for slot in (7, 8, 9, 10):
                apend[s, c, slot].wait_recv()
    for s in range(ns):
        for c in items(s):
            for slot in range(8):
                wire(s, c, slot).wait_send()
    for cp in sends + list(apend.values()):
        cp.wait_send()
    for cp in outs:
        cp.wait()


def tail(n, normal, across, wide, weights, m, v):
    side = math.isqrt(n // CORES)
    layers = weights[0].shape[0]
    shapes = [(t.shape[1], t.shape[2]) for t in m]
    slabs = tuple((k, l, *shapes[k]) for l in reversed(range(layers)) for k in ((0, 1, 2) if l == layers - 1 else (2, 0, 1)))
    weights = [t.reshape(layers, side, side, CORES, *shapes[k]) for k, t in enumerate(weights)]
    count = sum(layers * n * r * c for r, c in shapes)
    ns = len(slabs)
    tokens, ff = wide[0].shape
    d = normal[0].shape[1]
    sc = []
    for lead, dtype in (((side, side, CORES), BF16), ((side, side), BF16), ((), F32), ((), BF16), ((), F32), ((), F32), ((), BF16)):
        sc += [pltpu.VMEM((*lead, r, c), dtype) for _, _, r, c in slabs]
    pieces = [2 if k == 2 else side for k, _, _, _ in slabs]
    sc += [pltpu.VMEM((i, 3, side, r, c // i), BF16) for i, (_, _, r, c) in zip(pieces, slabs)]
    sc += [pltpu.VMEM((i, 6, r, c // i), BF16) for i, (_, _, r, c) in zip(pieces, slabs)]
    small = 1 + 2 * (side - 1)
    sc += [
        pltpu.VMEM((d, tokens), BF16),
        pltpu.VMEM((tokens, d), BF16),
        pltpu.VMEM((3, tokens, ff // side), BF16),
        pltpu.VMEM((4, 8, 128), F32),
        pltpu.VMEM((small, 8, 128), F32),
        pltpu.SemaphoreType.DMA((ns, side, 8)),
        pltpu.SemaphoreType.DMA((ns, side, 8)),
        pltpu.SemaphoreType.DMA((ns, 2, 11)),
        pltpu.SemaphoreType.DMA((ns, 2, 11)),
        pltpu.SemaphoreType.DMA((ns, 3)),
        pltpu.SemaphoreType.DMA((small,)),
        pltpu.SemaphoreType.DMA((small,)),
        pltpu.SemaphoreType.DMA((ns, 3)),
        pltpu.SemaphoreType.DMA((2,)),
        pltpu.SemaphoreType.DMA((3,)),
    ]
    out = [jax.ShapeDtypeStruct(t.shape, BF16) for t in weights]
    out += [jax.ShapeDtypeStruct(t.shape, F32) for t in (*m, *v)]
    ins = (*across, *normal, *wide, *weights, *m, *v)
    got = pl.pallas_call(
        functools.partial(tail_kernel, n, slabs, count),
        out_shape=out,
        in_specs=[ANY] * len(ins),
        out_specs=[ANY] * 9,
        scratch_shapes=sc,
        compiler_params=pltpu.CompilerParams(collective_id=0, has_side_effects=True, vmem_limit_bytes=67043328),
        name="tail",
    )(*ins)
    new = [t.reshape(layers, -1, t.shape[-1]) for t in got[:3]]
    return (*new, *got[3:])


def solution(mesh):
    n = mesh.shape["dp"]

    def step(x, dy, *arrays):
        weights, m, v = (arrays[i : i + 3] for i in (0, 3, 6))
        act0, act1, dg1, du1, dg0, du0, at0, at1, dh = states(x, dy, weights)
        return tail(n, (dh, dy[0]), (at0, at1), (dg0, dg1, du0, du1, act0, act1), weights, m, v)

    seq, whole, rows = P(("rep", "dp")), P(), P(None, "dp")
    return jax.shard_map(
        step,
        mesh=mesh,
        in_specs=(seq, seq, *[whole] * 3, *[rows] * 6),
        out_specs=(*[P("rep")] * 3, *[P("rep", "dp")] * 6),
        check_vma=False,
    )
```

profile of v0, /device:TPU:97, one launch (start us, length us, event | category | flops | bytes accessed | tf_op | source)
XLA Modules:
  0.0 256.8 jit_solution(8067808369922039857)
XLA Ops:
  0.6 86.5 %states.1 = (bf16[2048,2048]{1,0:T(8,128)(2,1)}, bf16[2048,2048]{1,0:T(8,128)(2,1)}, bf16[2048,2048]{1,0:T(8,128)(2,1)}, bf16[2048,2048]{1,0:T(8,128)(2,1)}, bf1...) custom-call(bf16[1,2048,768]{2,1,0:T(8,128)(2,1)} %refs_0_.1, ...), custom_call_target="tpu_custom_call" | custom-call | flops 57982058496 | bytes 104857600 | tf_op jit(solution)/shard_map/states/pallas_call | solution.py:152
  87.1 152.0 %tail.1 = (bf16[2,4,4,2,24,2048]{5,4,3,2,1,0:T(8,128)(2,1)}, bf16[2,4,4,2,24,2048]{5,4,3,2,1,0:T(8,128)(2,1)}, bf16[2,4,4,2,64,768]{5,4,3,2,1,0:T(8,128)(2,1)}, ...) custom-call(bf16[768,2048]{1,0:T(8,128)(2,1)} %get-tuple-element.27., ...), custom_call_target="tpu_custom_call" | custom-call | tf_op jit(solution)/shard_map/tail/pallas_call | solution.py:563
  239.1 0.0 copy-start
  239.1 0.0 slice-start
  239.1 7.0 %copy.29 = bf16[2,768,2048]{2,1,0:T(8,128)(2,1)} copy(bf16[2,768,2048]{2,1,0:T(8,128)(2,1)} %bitcast.14) | data formatting | bytes 12582912
  246.2 0.0 copy-done
  246.2 2.8 %copy.30 = bf16[2,768,2048]{2,1,0:T(8,128)(2,1)} copy(bf16[2,768,2048]{2,1,0:T(8,128)(2,1)S(1)} %bitcast.13) | data formatting | bytes 12582912
  249.0 0.0 slice-done
  249.0 0.4 slice-done.1
  249.4 0.0 copy-start.2
  249.4 0.0 copy-start.1
  249.4 2.9 %copy.31 = bf16[2,2048,768]{2,1,0:T(8,128)(2,1)} copy(bf16[2,2048,768]{2,1,0:T(8,128)(2,1)S(1)} %bitcast.12) | data formatting | bytes 12582912
  252.3 0.0 copy-done.6
  252.3 0.7 copy.32
  253.0 0.0 copy-done.5
  253.0 0.7 copy.33
  253.8 0.0 copy-done.4
  253.8 0.7 copy.34
  254.5 0.0 copy-done.3
  254.5 0.7 copy.35
  255.3 0.0 copy-done.2
  255.3 0.7 copy.36
  256.0 0.0 copy-done.1
  256.0 0.7 copy.37
  (6 shorter events, 0.0 us)
Async XLA Ops:
  239.1 7.1 %copy-start = (bf16[2,4,4,2,24,2048]{5,4,3,2,1,0:T(8,128)(2,1)S(1)}, bf16[2,4,4,2,24,2048]{5,4,3,2,1,0:T(8,128)(2,1)}, u32[]{:S(2)}) copy-start(bf16[2,4,4,2,24,2048]{5,4,3,2,1,0:T(8,128)(2,1)} %get-tuple-element.37) | copy-start | bytes 18874372
  239.1 9.9 %slice-start = ((s8[6291456]{0:T(1024)(128)(4,1)}), s8[4194304]{0:T(1024)(128)(4,1)S(1)}, s32[]{:S(2)}) async-start(s8[6291456]{0:T(1024)(128)(4,1)} %bitcast.10), calls=%async_computation | async-start | bytes 8388608
  246.2 3.2 %slice-start.1 = ((s8[6291456]{0:T(1024)(128)(4,1)}), s8[2097152]{0:T(1024)(128)(4,1)S(1)}, s32[]{:S(2)}) async-start(s8[6291456]{0:T(1024)(128)(4,1)} %bitcast.10), calls=%async_computation.1 | async-start | bytes 4194304
  249.4 2.9 %copy-start.6 = (f32[2,24,2048]{2,1,0:T(8,128)S(1)}, f32[2,24,2048]{2,1,0:T(8,128)}, u32[]{:S(2)}) copy-start(f32[2,24,2048]{2,1,0:T(8,128)} %get-tuple-element.57) | copy-start | bytes 1179652
  249.4 3.7 %copy-start.5 = (f32[2,24,2048]{2,1,0:T(8,128)S(1)}, f32[2,24,2048]{2,1,0:T(8,128)}, u32[]{:S(2)}) copy-start(f32[2,24,2048]{2,1,0:T(8,128)} %get-tuple-element.58) | copy-start | bytes 1179652
  249.4 4.4 %copy-start.4 = (f32[2,64,768]{2,1,0:T(8,128)S(1)}, f32[2,64,768]{2,1,0:T(8,128)}, u32[]{:S(2)}) copy-start(f32[2,64,768]{2,1,0:T(8,128)} %get-tuple-element.59) | copy-start | bytes 1179652
  249.4 5.2 %copy-start.3 = (f32[2,24,2048]{2,1,0:T(8,128)S(1)}, f32[2,24,2048]{2,1,0:T(8,128)}, u32[]{:S(2)}) copy-start(f32[2,24,2048]{2,1,0:T(8,128)} %get-tuple-element.60) | copy-start | bytes 1179652
  249.4 5.9 %copy-start.2 = (f32[2,24,2048]{2,1,0:T(8,128)S(1)}, f32[2,24,2048]{2,1,0:T(8,128)}, u32[]{:S(2)}) copy-start(f32[2,24,2048]{2,1,0:T(8,128)} %get-tuple-element.61) | copy-start | bytes 1179652
  249.4 6.7 %copy-start.1 = (f32[2,64,768]{2,1,0:T(8,128)S(1)}, f32[2,64,768]{2,1,0:T(8,128)}, u32[]{:S(2)}) copy-start(f32[2,64,768]{2,1,0:T(8,128)} %get-tuple-element.62) | copy-start | bytes 1179652
where the time goes:
time: 257 us
  Pallas kernels  238 us (93%)
  local copies, waits for them, and re-layouts  17.6 us (7%)
    pallas_call x1, Pallas kernels, tail(): pl.pallas_call(functools.partial(tail_kernel, n, slabs, count), out_shape...  152 us
    pallas_call x1, Pallas kernels, states(): pl.pallas_call(functools.partial(states_body, steps, min(512, ff)), grid=...  86.5 us
    unnamed x27, local copies, waits for them, and re-layouts  17.6 us

commit v1 on v0

--- a/solution.py
+++ b/solution.py
@@ -13,7 +13,7 @@
 ANY = pl.BlockSpec(memory_space=pl.ANY)
 VM = pl.BlockSpec(memory_space=pltpu.VMEM)
 CORES = 2
-LAGS = (0, 2, 5, 9, 12, 15)
+LAGS = (0, 2, 5, 10, 13, 17)
 
 
 def contract(a, b, dims):

time: 257 us -> 256 us (level)
  no operation moved by 1% of the time
where the time goes in v1:
time: 256 us
  Pallas kernels  238 us (93%)
  local copies, waits for them, and re-layouts  17.6 us (7%)
    pallas_call x1, Pallas kernels, tail(): pl.pallas_call(functools.partial(tail_kernel, n, slabs, count), out_shape...  151 us
    pallas_call x1, Pallas kernels, states(): pl.pallas_call(functools.partial(states_body, steps, min(512, ff)), grid=...  86.5 us
    unnamed x27, local copies, waits for them, and re-layouts  17.6 us

profile of v1, /device:TPU:97, one launch (start us, length us, event | category | flops | bytes accessed | tf_op | source)
XLA Modules:
  0.0 256.3 jit_solution(6291953126813978253)
XLA Ops:
  0.6 86.5 %states.1 = (bf16[2048,2048]{1,0:T(8,128)(2,1)}, bf16[2048,2048]{1,0:T(8,128)(2,1)}, bf16[2048,2048]{1,0:T(8,128)(2,1)}, bf16[2048,2048]{1,0:T(8,128)(2,1)}, bf1...) custom-call(bf16[1,2048,768]{2,1,0:T(8,128)(2,1)} %refs_0_.1, ...), custom_call_target="tpu_custom_call" | custom-call | flops 57982058496 | bytes 104857600 | tf_op jit(solution)/shard_map/states/pallas_call | solution.py:152
  87.1 151.5 %tail.1 = (bf16[2,4,4,2,24,2048]{5,4,3,2,1,0:T(8,128)(2,1)}, bf16[2,4,4,2,24,2048]{5,4,3,2,1,0:T(8,128)(2,1)}, bf16[2,4,4,2,64,768]{5,4,3,2,1,0:T(8,128)(2,1)}, ...) custom-call(bf16[768,2048]{1,0:T(8,128)(2,1)} %get-tuple-element.27., ...), custom_call_target="tpu_custom_call" | custom-call | tf_op jit(solution)/shard_map/tail/pallas_call | solution.py:563
  238.6 0.0 copy-start
  238.7 0.0 slice-start
  238.7 7.0 %copy.29 = bf16[2,768,2048]{2,1,0:T(8,128)(2,1)} copy(bf16[2,768,2048]{2,1,0:T(8,128)(2,1)} %bitcast.14) | data formatting | bytes 12582912
  245.7 0.0 copy-done
  245.7 2.8 %copy.30 = bf16[2,768,2048]{2,1,0:T(8,128)(2,1)} copy(bf16[2,768,2048]{2,1,0:T(8,128)(2,1)S(1)} %bitcast.13) | data formatting | bytes 12582912
  248.5 0.0 slice-done
  248.5 0.4 slice-done.1
  248.9 0.0 copy-start.2
  248.9 0.0 copy-start.1
  248.9 2.9 %copy.31 = bf16[2,2048,768]{2,1,0:T(8,128)(2,1)} copy(bf16[2,2048,768]{2,1,0:T(8,128)(2,1)S(1)} %bitcast.12) | data formatting | bytes 12582912
  251.8 0.0 copy-done.6
  251.8 0.7 copy.32
  252.6 0.0 copy-done.5
  252.6 0.7 copy.33
  253.3 0.0 copy-done.4
  253.3 0.7 copy.34
  254.1 0.0 copy-done.3
  254.1 0.7 copy.35
  254.8 0.0 copy-done.2
  254.8 0.7 copy.36
  255.6 0.0 copy-done.1
  255.6 0.7 copy.37
  (6 shorter events, 0.0 us)
Async XLA Ops:
  238.6 7.1 %copy-start = (bf16[2,4,4,2,24,2048]{5,4,3,2,1,0:T(8,128)(2,1)S(1)}, bf16[2,4,4,2,24,2048]{5,4,3,2,1,0:T(8,128)(2,1)}, u32[]{:S(2)}) copy-start(bf16[2,4,4,2,24,2048]{5,4,3,2,1,0:T(8,128)(2,1)} %get-tuple-element.37) | copy-start | bytes 18874372
  238.7 9.9 %slice-start = ((s8[6291456]{0:T(1024)(128)(4,1)}), s8[4194304]{0:T(1024)(128)(4,1)S(1)}, s32[]{:S(2)}) async-start(s8[6291456]{0:T(1024)(128)(4,1)} %bitcast.10), calls=%async_computation | async-start | bytes 8388608
  245.7 3.2 %slice-start.1 = ((s8[6291456]{0:T(1024)(128)(4,1)}), s8[2097152]{0:T(1024)(128)(4,1)S(1)}, s32[]{:S(2)}) async-start(s8[6291456]{0:T(1024)(128)(4,1)} %bitcast.10), calls=%async_computation.1 | async-start | bytes 4194304
  248.9 2.9 %copy-start.6 = (f32[2,24,2048]{2,1,0:T(8,128)S(1)}, f32[2,24,2048]{2,1,0:T(8,128)}, u32[]{:S(2)}) copy-start(f32[2,24,2048]{2,1,0:T(8,128)} %get-tuple-element.57) | copy-start | bytes 1179652
  248.9 3.7 %copy-start.5 = (f32[2,24,2048]{2,1,0:T(8,128)S(1)}, f32[2,24,2048]{2,1,0:T(8,128)}, u32[]{:S(2)}) copy-start(f32[2,24,2048]{2,1,0:T(8,128)} %get-tuple-element.58) | copy-start | bytes 1179652
  248.9 4.4 %copy-start.4 = (f32[2,64,768]{2,1,0:T(8,128)S(1)}, f32[2,64,768]{2,1,0:T(8,128)}, u32[]{:S(2)}) copy-start(f32[2,64,768]{2,1,0:T(8,128)} %get-tuple-element.59) | copy-start | bytes 1179652
  248.9 5.2 %copy-start.3 = (f32[2,24,2048]{2,1,0:T(8,128)S(1)}, f32[2,24,2048]{2,1,0:T(8,128)}, u32[]{:S(2)}) copy-start(f32[2,24,2048]{2,1,0:T(8,128)} %get-tuple-element.60) | copy-start | bytes 1179652
  248.9 5.9 %copy-start.2 = (f32[2,24,2048]{2,1,0:T(8,128)S(1)}, f32[2,24,2048]{2,1,0:T(8,128)}, u32[]{:S(2)}) copy-start(f32[2,24,2048]{2,1,0:T(8,128)} %get-tuple-element.61) | copy-start | bytes 1179652
  248.9 6.7 %copy-start.1 = (f32[2,64,768]{2,1,0:T(8,128)S(1)}, f32[2,64,768]{2,1,0:T(8,128)}, u32[]{:S(2)}) copy-start(f32[2,64,768]{2,1,0:T(8,128)} %get-tuple-element.62) | copy-start | bytes 1179652
